TPU v7x, 32 devices: a whole 2x2x4 slice. The times are simulated.
32 devices in a mesh: head: 4 (over x, core), inner: 2 (over y), outer: 4 (over z).
Axes of the slice: x: 2, y: 2, z: 4, core: 2. Of those that a mesh axis runs over, the one named last changes fastest.
Arguments:
- rotated_asking_matrix: bfloat16 [4096, 32, 128], P(('head', 'inner', 'outer')), may hold values from -12 to 12
- rotated_lookup_matrix: bfloat16 [4096, 8, 128], P(('head', 'inner', 'outer')), may hold values from -6 to 6
- content_matrix: bfloat16 [4096, 8, 128], P(('head', 'inner', 'outer')), may hold values from -6 to 6
Outputs:
- attended: bfloat16 [4096, 32, 128], P(('head', 'inner', 'outer'))
All inputs are finite; a program needn't handle non-finite values.
Results may differ from a plain program's by a relative error of at most 0.001.
Values may be sent and summed in bfloat16 or wider, within the bound.
A program may use at most 64 MiB of HBM per device.

v0:
```python
import math
import jax
import jax.numpy as jnp
from jax import lax
from jax.sharding import PartitionSpec as P


def for_sending(x):

    def short(part):
        return part.astype(jnp.bfloat16) if part.dtype == jnp.float32 else part

    return jax.tree.map(short, x)


def passed_along(x, axis, by):
    size = lax.axis_size(axis)
    return lax.ppermute(x, axis, [(i, (i + by) % size) for i in range(size)])


def shards(rotated_asking_matrix, rotated_lookup_matrix, content_matrix):
    query_local, key_local, value_local = (
        lax.all_to_all(rotated_asking_matrix, "head", split_axis=1, concat_axis=0, tiled=True),
        lax.all_to_all(rotated_lookup_matrix, "head", split_axis=1, concat_axis=0, tiled=True),
        lax.all_to_all(content_matrix, "head", split_axis=1, concat_axis=0, tiled=True),
    )
    inner_count = lax.axis_size("inner")
    outer_count = lax.axis_size("outer")
    cycle_count = inner_count * outer_count
    block_len = rotated_asking_matrix.shape[0]
    local_len = key_local.shape[0]
    kv_heads = key_local.shape[1]
    group_size = query_local.shape[1] // kv_heads
    head_dim = query_local.shape[2]
    grouped = query_local.reshape(local_len, kv_heads, group_size, head_dim)
    inner_self = lax.axis_index("inner")
    outer_self = lax.axis_index("outer")
    offsets = jnp.arange(local_len, dtype=jnp.int32)
    score_scale = 1.0 / math.sqrt(head_dim)

    def places(cycle_id):
        return (offsets // block_len * cycle_count + cycle_id) * block_len + offsets % block_len

    query_pos = places(inner_self * outer_count + outer_self)

    def absorb(carry, key_block, value_block, key_pos):
        run_max, run_sum, accum = carry
        scores = (
            jnp.einsum("tkgd,skd->kgts", grouped, key_block, preferred_element_type=jnp.float32)
            * score_scale
        )
        allowed = key_pos[None, :] <= query_pos[:, None]
        scores = jnp.where(allowed, scores, -1e30)
        new_max = jnp.maximum(run_max, jnp.max(scores, axis=-1))
        factor = jnp.exp(run_max - new_max)
        weights = jnp.where(allowed, jnp.exp(scores - new_max[..., None]), 0.0)
        run_sum = run_sum * factor + jnp.sum(weights, axis=-1)
        mixed = jnp.einsum(
            "kgts,skd->kgtd",
            weights,
            value_block.astype(jnp.float32),
            precision=lax.Precision.HIGHEST,
        )
        accum = accum * factor[..., None] + mixed
        return (new_max, run_sum, accum)

    def sweep(carry, window, outer_step):
        outer_source = (outer_self - outer_step) % outer_count

        def cycle_pos(inner_source):
            return places(inner_source * outer_count + outer_source)

        carry = absorb(carry, window[0], window[1], cycle_pos(inner_self))

        def inner_body(inner_step, loop_state):
            carry_state, moving = loop_state
            moving = jax.tree.map(
                lambda part, own: part.astype(own.dtype),
                passed_along(for_sending(moving), "inner", 1),
                moving,
            )
            key_pos = cycle_pos((inner_self - inner_step) % inner_count)
            carry_state = absorb(carry_state, moving[0], moving[1], key_pos)
            return (carry_state, moving)

        carry, moving = lax.fori_loop(1, inner_count, inner_body, (carry, window))
        return carry

    carry = (
        jnp.full((kv_heads, group_size, local_len), -1e30, jnp.float32),
        jnp.zeros((kv_heads, group_size, local_len), jnp.float32),
        jnp.zeros((kv_heads, group_size, local_len, head_dim), jnp.float32),
    )
    window = jnp.stack([key_local, value_local])

    def outer_body(outer_step, loop_state):
        carry_state, current = loop_state
        upcoming = jax.tree.map(
            lambda part, own: part.astype(own.dtype),
            passed_along(for_sending(current), "outer", 1),
            current,
        )
        carry_state = sweep(carry_state, current, outer_step)
        return (carry_state, upcoming)

    carry, window = lax.fori_loop(0, outer_count - 1, outer_body, (carry, window))
    carry = sweep(carry, window, outer_count - 1)
    run_max, run_sum, accum = carry
    result = (accum / run_sum[..., None]).astype(jnp.bfloat16)
    result = result.transpose(2, 0, 1, 3).reshape(local_len, kv_heads * group_size, head_dim)
    return lax.all_to_all(result, "head", split_axis=0, concat_axis=1, tiled=True)


def solution(mesh):
    placed = (
        P(("head", "inner", "outer"), None, None),
        P(("head", "inner", "outer"), None, None),
        P(("head", "inner", "outer"), None, None),
    )
    return jax.shard_map(
        shards,
        mesh=mesh,
        in_specs=placed,
        out_specs=P(("head", "inner", "outer"), None, None),
        check_vma=False,
    )
```

profile of v0, /device:TPU:0, one launch (start us, length us, event | category | flops | bytes accessed | tf_op | source)
XLA Modules:
  0.0 204.6 jit_solution(4616779751320213047)
XLA Ops:
  0.0 1.7 copy.14
  1.7 4.2 %all-to-all-start = ((bf16[128,8,128]{2,0,1:T(8,128)(2,1)}), bf16[128,8,128]{2,0,1:T(8,128)(2,1)S(1)}, u32[]{:S(2)}, u32[]{:S(2)}) async-start(bf16[128,8,128]{2,0,1:T(8,128)(2,1)} %copy.14), calls=%async_computation | async-start | bytes 524288 | tf_op jit(solution)/shard_map/all_to_all | solution.py:24
  5.9 1.7 copy.16
  7.6 4.3 %all-to-all-done = bf16[128,8,128]{2,0,1:T(8,128)(2,1)S(1)} async-done(((bf16[128,8,128]{2,0,1:T(8,128)(2,1)}), bf16[128,8,128]{2,0,1:T(8,128)(2,1)S(1)}, u32[]{:S(2)}, u32[]{:S(2)}) %all-to-all-start) | async-done | bytes 262176 | tf_op jit(solution)/shard_map/all_to_all | solution.py:24
  11.9 3.4 %all-to-all-start.1 = ((bf16[128,8,128]{2,0,1:T(8,128)(2,1)}), bf16[128,8,128]{2,0,1:T(8,128)(2,1)S(1)}, u32[]{:S(2)}, u32[]{:S(2)}) async-start(bf16[128,8,128]{2,0,1:T(8,128)(2,1)} %copy.16), calls=%async_computation.1 | async-start | bytes 524288 | tf_op jit(solution)/shard_map/all_to_all | solution.py:25
  15.3 2.6 %copy.18 = bf16[128,32,128]{2,0,1:T(8,128)(2,1)} copy(bf16[128,32,128]{2,1,0:T(8,128)(2,1)} %param.5) | data formatting | bytes 2097152 | tf_op args[0]
  17.9 3.4 %all-to-all-done.1 = bf16[128,8,128]{2,0,1:T(8,128)(2,1)S(1)} async-done(((bf16[128,8,128]{2,0,1:T(8,128)(2,1)}), bf16[128,8,128]{2,0,1:T(8,128)(2,1)S(1)}, u32[]{:S(2)}, u32[]{:S(2)}) %all-to-all-start.1) | async-done | bytes 262176 | tf_op jit(solution)/shard_map/all_to_all | solution.py:25
  21.3 3.5 %all-to-all-start.2 = ((bf16[128,32,128]{2,0,1:T(8,128)(2,1)}), bf16[128,32,128]{2,0,1:T(8,128)(2,1)S(1)}, u32[]{:S(2)}, u32[]{:S(2)}) async-start(bf16[128,32,128]{2,0,1:T(8,128)(2,1)} %copy.18), calls=%async_computation.2 | async-start | bytes 2097152 | tf_op jit(solution)/shard_map/all_to_all | solution.py:23
  25.1 14.2 %all-to-all-done.2 = bf16[128,32,128]{2,0,1:T(8,128)(2,1)S(1)} async-done(((bf16[128,32,128]{2,0,1:T(8,128)(2,1)}), bf16[128,32,128]{2,0,1:T(8,128)(2,1)S(1)}, u32[]{:S(2)}, u32[]{:S(2)}) %all-to-all-start.2) | async-done | bytes 1048608 | tf_op jit(solution)/shard_map/all_to_all | solution.py:23
  39.3 111.7 %while.49 = (s32[]{:T(128)}, f32[2,4,512]{2,1,0:T(4,128)S(1)}, f32[2,4,512]{2,1,0:T(4,128)S(1)}, f32[2,4,512,128]{3,2,1,0:T(8,128)}, bf16[2,512,2,128]{3,1,2,0:T...) while((s32[]{:T(128)}, f32[2,4,512]{2,1,0:T(4,128)S(1)}, ...), condition=%wide.region_5.6_spmd.clone.clone, body=%wide.region_0.5_spmd.clone.clone.sunk | while | flops 7569716736 | bytes 86422968 | solution.py:106
  39.4 2.2 %collective-permute-start = (bf16[2,512,2,128]{3,1,2,0:T(8,128)(2,1)S(1)}, bf16[2,512,2,128]{3,1,2,0:T(8,128)(2,1)S(1)}, u32[]{:S(2)}, u32[]{:S(2)}) collective-permute-start(bf16[2,512,2,128]{3,1,2,0:T(8,128)(2,1)S(1)} %copy.47), channel_id=1, source_target_pairs={{0,4},{4,0},{1,5},{5,1},{2,6},{6,2},{3,7},{7,3},{8,12},{12,8},{9,1... | collective-permute-start | bytes 1572872 | tf_op jit(solution)/shard_map/while/body/eval_jaxpr/while/body/eval_jaxpr/ppermute | solution.py:18
  41.6 1.6 collective-permute-start.1
  45.2 8.1 %collective-permute-done = bf16[2,512,2,128]{3,1,2,0:T(8,128)(2,1)S(1)} collective-permute-done((bf16[2,512,2,128]{3,1,2,0:T(8,128)(2,1)S(1)}, bf16[2,512,2,128]{3,1,2,0:T(8,128)(2,1)S(1)}, u32[]{:S(2)}, u32[]{:S(2)}) %collective-permute-start) | collective-permute-done | bytes 524320 | tf_op jit(solution)/shard_map/while/body/eval_jaxpr/while/body/eval_jaxpr/ppermute | solution.py:18
  54.8 7.6 %fusion.117 = f32[2,4,512,128]{3,2,1,0:T(8,128)S(1)} fusion(f32[2,512,512,4]{2,1,3,0:T(8,128)S(1)} %get-tuple-element.740, f32[2,4,512]{2,1,0:T(4,128)S(1)} %get-tuple-element.741, pred[512,512]{0,1:T(8,128)(4,1)S(1)} %get-tuple-element.737, bf16[2,512,2,128]{3,1,2,0:T(8,128)(2,1)S(1)} %copy.47), kind=kOutput, calls=%fused_computation.11.clone.1 | convolution fusion | flops 3229614080 | bytes 11026432 | tf_op jit(solution)/shard_map/while/body/eval_jaxpr/kgts,skd->kgtd/dot_general | solution.py:58
  62.4 4.1 %fusion.115 = (f32[2,4,512]{2,1,0:T(4,128)S(1)}, f32[2,4,512]{2,1,0:T(4,128)S(1)}) fusion(f32[2,512,512,4]{2,1,3,0:T(8,128)S(1)} %get-tuple-element.740, f32[2,4,512]{2,1,0:T(4,128)S(1)} %get-tuple-element.741, pred[512,512]{0,1:T(8,128)(4,1)S(1)} %get-tuple-element.737, f32[2,4,512]{2,1,0:T(4,128)S(1)} %get-tuple-element.777, ...), kind=kLoop, calls=%fused_computation.12.clone.1 | loop fusion | flops 20963328 | bytes 17367040 | tf_op jit(solution)/shard_map/while/body/eval_jaxpr/reduce_sum | solution.py:57
  66.5 9.6 %fusion.118 = f32[2,4,512,128]{3,2,1,0:T(8,128)S(1)} fusion(f32[2,4,512,128]{3,2,1,0:T(8,128)S(1)} %fusion.117, f32[2,4,512,128]{3,2,1,0:T(8,128)S(1)} %copy-done, f32[2,512,512,4]{2,1,3,0:T(8,128)S(1)} %get-tuple-element.742, f32[2,4,512]{2,1,0:T(4,128)S(1)} %get-tuple-element.777, pred[512,512]{0,1:T(8,128)(4,1)S(1)} %get-tuple-element.735, ...), kind=kOutput, calls=%fused_computation.28.clone.1 | convolution fusion | flops 3232235520 | bytes 15253505 | tf_op jit(solution)/shard_map/while/body/eval_jaxpr/while/body/eval_jaxpr/kgts,skd->kgtd/dot_general | solution.py:58
  77.5 1.8 collective-permute-start
  79.3 1.6 collective-permute-start.1
  82.9 7.5 %collective-permute-done = bf16[2,512,2,128]{3,1,2,0:T(8,128)(2,1)S(1)} collective-permute-done((bf16[2,512,2,128]{3,1,2,0:T(8,128)(2,1)S(1)}, bf16[2,512,2,128]{3,1,2,0:T(8,128)(2,1)S(1)}, u32[]{:S(2)}, u32[]{:S(2)}) %collective-permute-start) | collective-permute-done | bytes 524320 | tf_op jit(solution)/shard_map/while/body/eval_jaxpr/while/body/eval_jaxpr/ppermute | solution.py:18
  92.0 7.6 %fusion.117 = f32[2,4,512,128]{3,2,1,0:T(8,128)S(1)} fusion(f32[2,512,512,4]{2,1,3,0:T(8,128)S(1)} %get-tuple-element.740, f32[2,4,512]{2,1,0:T(4,128)S(1)} %get-tuple-element.741, pred[512,512]{0,1:T(8,128)(4,1)S(1)} %get-tuple-element.737, bf16[2,512,2,128]{3,1,2,0:T(8,128)(2,1)S(1)} %copy.47), kind=kOutput, calls=%fused_computation.11.clone.1 | convolution fusion | flops 3229614080 | bytes 11026432 | tf_op jit(solution)/shard_map/while/body/eval_jaxpr/kgts,skd->kgtd/dot_general | solution.py:58
  99.6 4.1 %fusion.115 = (f32[2,4,512]{2,1,0:T(4,128)S(1)}, f32[2,4,512]{2,1,0:T(4,128)S(1)}) fusion(f32[2,512,512,4]{2,1,3,0:T(8,128)S(1)} %get-tuple-element.740, f32[2,4,512]{2,1,0:T(4,128)S(1)} %get-tuple-element.741, pred[512,512]{0,1:T(8,128)(4,1)S(1)} %get-tuple-element.737, f32[2,4,512]{2,1,0:T(4,128)S(1)} %get-tuple-element.777, ...), kind=kLoop, calls=%fused_computation.12.clone.1 | loop fusion | flops 20963328 | bytes 17367040 | tf_op jit(solution)/shard_map/while/body/eval_jaxpr/reduce_sum | solution.py:57
  103.7 9.6 %fusion.118 = f32[2,4,512,128]{3,2,1,0:T(8,128)S(1)} fusion(f32[2,4,512,128]{3,2,1,0:T(8,128)S(1)} %fusion.117, f32[2,4,512,128]{3,2,1,0:T(8,128)S(1)} %copy-done, f32[2,512,512,4]{2,1,3,0:T(8,128)S(1)} %get-tuple-element.742, f32[2,4,512]{2,1,0:T(4,128)S(1)} %get-tuple-element.777, pred[512,512]{0,1:T(8,128)(4,1)S(1)} %get-tuple-element.735, ...), kind=kOutput, calls=%fused_computation.28.clone.1 | convolution fusion | flops 3232235520 | bytes 15253505 | tf_op jit(solution)/shard_map/while/body/eval_jaxpr/while/body/eval_jaxpr/kgts,skd->kgtd/dot_general | solution.py:58
  116.2 1.6 collective-permute-start.1
  119.8 6.9 %collective-permute-done = bf16[2,512,2,128]{3,1,2,0:T(8,128)(2,1)S(1)} collective-permute-done((bf16[2,512,2,128]{3,1,2,0:T(8,128)(2,1)S(1)}, bf16[2,512,2,128]{3,1,2,0:T(8,128)(2,1)S(1)}, u32[]{:S(2)}, u32[]{:S(2)}) %collective-permute-start) | collective-permute-done | bytes 524320 | tf_op jit(solution)/shard_map/while/body/eval_jaxpr/while/body/eval_jaxpr/ppermute | solution.py:18
  128.2 7.6 %fusion.117 = f32[2,4,512,128]{3,2,1,0:T(8,128)S(1)} fusion(f32[2,512,512,4]{2,1,3,0:T(8,128)S(1)} %get-tuple-element.740, f32[2,4,512]{2,1,0:T(4,128)S(1)} %get-tuple-element.741, pred[512,512]{0,1:T(8,128)(4,1)S(1)} %get-tuple-element.737, bf16[2,512,2,128]{3,1,2,0:T(8,128)(2,1)S(1)} %copy.47), kind=kOutput, calls=%fused_computation.11.clone.1 | convolution fusion | flops 3229614080 | bytes 11026432 | tf_op jit(solution)/shard_map/while/body/eval_jaxpr/kgts,skd->kgtd/dot_general | solution.py:58
  135.9 4.1 %fusion.115 = (f32[2,4,512]{2,1,0:T(4,128)S(1)}, f32[2,4,512]{2,1,0:T(4,128)S(1)}) fusion(f32[2,512,512,4]{2,1,3,0:T(8,128)S(1)} %get-tuple-element.740, f32[2,4,512]{2,1,0:T(4,128)S(1)} %get-tuple-element.741, pred[512,512]{0,1:T(8,128)(4,1)S(1)} %get-tuple-element.737, f32[2,4,512]{2,1,0:T(4,128)S(1)} %get-tuple-element.777, ...), kind=kLoop, calls=%fused_computation.12.clone.1 | loop fusion | flops 20963328 | bytes 17367040 | tf_op jit(solution)/shard_map/while/body/eval_jaxpr/reduce_sum | solution.py:57
  140.0 9.6 %fusion.118 = f32[2,4,512,128]{3,2,1,0:T(8,128)S(1)} fusion(f32[2,4,512,128]{3,2,1,0:T(8,128)S(1)} %fusion.117, f32[2,4,512,128]{3,2,1,0:T(8,128)S(1)} %copy-done, f32[2,512,512,4]{2,1,3,0:T(8,128)S(1)} %get-tuple-element.742, f32[2,4,512]{2,1,0:T(4,128)S(1)} %get-tuple-element.777, pred[512,512]{0,1:T(8,128)(4,1)S(1)} %get-tuple-element.735, ...), kind=kOutput, calls=%fused_computation.28.clone.1 | convolution fusion | flops 3232235520 | bytes 15253505 | tf_op jit(solution)/shard_map/while/body/eval_jaxpr/while/body/eval_jaxpr/kgts,skd->kgtd/dot_general | solution.py:58
  154.2 8.0 %collective-permute-done.2 = bf16[2,512,2,128]{3,1,2,0:T(8,128)(2,1)S(1)} collective-permute-done((bf16[2,512,2,128]{3,1,2,0:T(8,128)(2,1)S(1)}, bf16[2,512,2,128]{3,1,2,0:T(8,128)(2,1)S(1)}, u32[]{:S(2)}, u32[]{:S(2)}) %collective-permute-start.2) | collective-permute-done | bytes 524320 | tf_op jit(solution)/shard_map/while/body/eval_jaxpr/ppermute | solution.py:18
  163.8 7.6 %fusion.58 = f32[2,4,512,128]{3,2,1,0:T(8,128)S(1)} fusion(f32[2,512,512,4]{2,1,3,0:T(8,128)S(1)} %get-tuple-element.649, f32[2,4,512]{2,1,0:T(4,128)S(1)} %bitcast.171, pred[512,512]{0,1:T(8,128)(4,1)S(1)} %get-tuple-element.644, bf16[2,512,2,128]{3,1,2,0:T(8,128)(2,1)S(1)} %get-tuple-element.515), kind=kOutput, calls=%fused_computation.78 | convolution fusion | flops 3229614080 | bytes 11026432 | tf_op jit(solution)/shard_map/kgts,skd->kgtd/dot_general | solution.py:58
  171.4 4.3 %fusion.57 = (f32[2,4,512]{2,1,0:T(4,128)S(1)}, f32[2,4,512]{2,1,0:T(4,128)S(1)}) fusion(f32[2,512,512,4]{2,1,3,0:T(8,128)S(1)} %get-tuple-element.649, f32[2,4,512]{2,1,0:T(4,128)S(1)} %bitcast.172, pred[512,512]{0,1:T(8,128)(4,1)S(1)} %get-tuple-element.644, f32[2,4,512]{2,1,0:T(4,128)S(1)} %bitcast.169, f32[2,512,512,4]{2,1,3,0:T(8,128)S(1)} %get-tuple-element.647, ...), kind=kLoop, calls=%fused_computation.77 | loop fusion | flops 20963328 | bytes 17367040 | tf_op jit(solution)/shard_map/reduce_sum | solution.py:57
  175.7 9.4 %divide_convert_fusion = bf16[2,4,512,128]{3,2,1,0:T(8,128)(2,1)S(1)} fusion(f32[2,4,512,128]{3,2,1,0:T(8,128)S(1)} %fusion.58, f32[2,4,512,128]{3,2,1,0:T(8,128)S(1)} %copy-done.2, f32[2,512,512,4]{2,1,3,0:T(8,128)S(1)} %get-tuple-element.647, f32[2,4,512]{2,1,0:T(4,128)S(1)} %bitcast.170, pred[512,512]{0,1:T(8,128)(4,1)S(1)} %get-tuple-element.645, ...), kind=kOutput, calls=%fused_computation.91 | convolution fusion | flops 3232759808 | bytes 14221312 | tf_op jit(solution)/shard_map/while/body/eval_jaxpr/kgts,skd->kgtd/dot_general | solution.py:58
  185.8 17.4 %all_to_all.63 = bf16[512,8,128]{2,1,0:T(8,128)(2,1)S(1)} all-to-all(bf16[512,8,128]{2,1,0:T(8,128)(2,1)S(1)} %copy.22), channel_id=1, replica_groups=mesh['head'=4,'inner'=2,'outer'=4] {'head'}, dimensions={0} | all-to-all | bytes 2097152 | tf_op jit(solution)/shard_map/all_to_all | solution.py:111
  (66 shorter events, 23.0 us)
Async XLA Ops:
  1.7 10.2 %all-to-all-start = ((bf16[128,8,128]{2,0,1:T(8,128)(2,1)}), bf16[128,8,128]{2,0,1:T(8,128)(2,1)S(1)}, u32[]{:S(2)}, u32[]{:S(2)}) async-start(bf16[128,8,128]{2,0,1:T(8,128)(2,1)} %copy.14), calls=%async_computation | async-start | bytes 524288 | tf_op jit(solution)/shard_map/all_to_all | solution.py:24
  11.9 9.4 %all-to-all-start.1 = ((bf16[128,8,128]{2,0,1:T(8,128)(2,1)}), bf16[128,8,128]{2,0,1:T(8,128)(2,1)S(1)}, u32[]{:S(2)}, u32[]{:S(2)}) async-start(bf16[128,8,128]{2,0,1:T(8,128)(2,1)} %copy.16), calls=%async_computation.1 | async-start | bytes 524288 | tf_op jit(solution)/shard_map/all_to_all | solution.py:25
  21.3 17.9 %all-to-all-start.2 = ((bf16[128,32,128]{2,0,1:T(8,128)(2,1)}), bf16[128,32,128]{2,0,1:T(8,128)(2,1)S(1)}, u32[]{:S(2)}, u32[]{:S(2)}) async-start(bf16[128,32,128]{2,0,1:T(8,128)(2,1)} %copy.18), calls=%async_computation.2 | async-start | bytes 2097152 | tf_op jit(solution)/shard_map/all_to_all | solution.py:23
  39.4 13.8 %collective-permute-start = (bf16[2,512,2,128]{3,1,2,0:T(8,128)(2,1)S(1)}, bf16[2,512,2,128]{3,1,2,0:T(8,128)(2,1)S(1)}, u32[]{:S(2)}, u32[]{:S(2)}) collective-permute-start(bf16[2,512,2,128]{3,1,2,0:T(8,128)(2,1)S(1)} %copy.47), channel_id=1, source_target_pairs={{0,4},{4,0},{1,5},{5,1},{2,6},{6,2},{3,7},{7,3},{8,12},{12,8},{9,1... | collective-permute-start | bytes 1572872 | tf_op jit(solution)/shard_map/while/body/eval_jaxpr/while/body/eval_jaxpr/ppermute | solution.py:18
  41.6 34.5 %collective-permute-start.1 = (bf16[2,512,2,128]{3,1,2,0:T(8,128)(2,1)S(1)}, bf16[2,512,2,128]{3,1,2,0:T(8,128)(2,1)S(1)}, u32[]{:S(2)}, u32[]{:S(2)}) collective-permute-start(bf16[2,512,2,128]{3,1,2,0:T(8,128)(2,1)S(1)} %copy.47), channel_id=1, source_target_pairs={{0,1},{1,2},{2,3},{3,0},{4,5},{5,6},{6,7},{7,4},{8,9},{9,10},{10,1... | collective-permute-start | bytes 1572872 | tf_op jit(solution)/shard_map/while/body/eval_jaxpr/ppermute | solution.py:18
  62.4 4.1 %copy-start = (f32[2,4,512,128]{3,2,1,0:T(8,128)S(1)}, f32[2,4,512,128]{3,2,1,0:T(8,128)}, u32[]{:S(2)}) copy-start(f32[2,4,512,128]{3,2,1,0:T(8,128)} %get-tuple-element.765) | copy-start | bytes 6291460 | tf_op jit(solution)/shard_map/while
  76.1 1.4 copy-start.1
  77.5 12.9 %collective-permute-start = (bf16[2,512,2,128]{3,1,2,0:T(8,128)(2,1)S(1)}, bf16[2,512,2,128]{3,1,2,0:T(8,128)(2,1)S(1)}, u32[]{:S(2)}, u32[]{:S(2)}) collective-permute-start(bf16[2,512,2,128]{3,1,2,0:T(8,128)(2,1)S(1)} %copy.47), channel_id=1, source_target_pairs={{0,4},{4,0},{1,5},{5,1},{2,6},{6,2},{3,7},{7,3},{8,12},{12,8},{9,1... | collective-permute-start | bytes 1572872 | tf_op jit(solution)/shard_map/while/body/eval_jaxpr/while/body/eval_jaxpr/ppermute | solution.py:18
  79.3 34.0 %collective-permute-start.1 = (bf16[2,512,2,128]{3,1,2,0:T(8,128)(2,1)S(1)}, bf16[2,512,2,128]{3,1,2,0:T(8,128)(2,1)S(1)}, u32[]{:S(2)}, u32[]{:S(2)}) collective-permute-start(bf16[2,512,2,128]{3,1,2,0:T(8,128)(2,1)S(1)} %copy.47), channel_id=1, source_target_pairs={{0,1},{1,2},{2,3},{3,0},{4,5},{5,6},{6,7},{7,4},{8,9},{9,10},{10,1... | collective-permute-start | bytes 1572872 | tf_op jit(solution)/shard_map/while/body/eval_jaxpr/ppermute | solution.py:18
  99.6 4.1 %copy-start = (f32[2,4,512,128]{3,2,1,0:T(8,128)S(1)}, f32[2,4,512,128]{3,2,1,0:T(8,128)}, u32[]{:S(2)}) copy-start(f32[2,4,512,128]{3,2,1,0:T(8,128)} %get-tuple-element.765) | copy-start | bytes 6291460 | tf_op jit(solution)/shard_map/while
  113.3 1.4 copy-start.1
  114.7 12.0 %collective-permute-start = (bf16[2,512,2,128]{3,1,2,0:T(8,128)(2,1)S(1)}, bf16[2,512,2,128]{3,1,2,0:T(8,128)(2,1)S(1)}, u32[]{:S(2)}, u32[]{:S(2)}) collective-permute-start(bf16[2,512,2,128]{3,1,2,0:T(8,128)(2,1)S(1)} %copy.47), channel_id=1, source_target_pairs={{0,4},{4,0},{1,5},{5,1},{2,6},{6,2},{3,7},{7,3},{8,12},{12,8},{9,1... | collective-permute-start | bytes 1572872 | tf_op jit(solution)/shard_map/while/body/eval_jaxpr/while/body/eval_jaxpr/ppermute | solution.py:18
  116.2 33.4 %collective-permute-start.1 = (bf16[2,512,2,128]{3,1,2,0:T(8,128)(2,1)S(1)}, bf16[2,512,2,128]{3,1,2,0:T(8,128)(2,1)S(1)}, u32[]{:S(2)}, u32[]{:S(2)}) collective-permute-start(bf16[2,512,2,128]{3,1,2,0:T(8,128)(2,1)S(1)} %copy.47), channel_id=1, source_target_pairs={{0,1},{1,2},{2,3},{3,0},{4,5},{5,6},{6,7},{7,4},{8,9},{9,10},{10,1... | collective-permute-start | bytes 1572872 | tf_op jit(solution)/shard_map/while/body/eval_jaxpr/ppermute | solution.py:18
  135.9 4.1 %copy-start = (f32[2,4,512,128]{3,2,1,0:T(8,128)S(1)}, f32[2,4,512,128]{3,2,1,0:T(8,128)}, u32[]{:S(2)}) copy-start(f32[2,4,512,128]{3,2,1,0:T(8,128)} %get-tuple-element.765) | copy-start | bytes 6291460 | tf_op jit(solution)/shard_map/while
  149.6 1.4 copy-start.1
  151.1 11.1 %collective-permute-start.2 = (bf16[2,512,2,128]{3,1,2,0:T(8,128)(2,1)S(1)}, bf16[2,512,2,128]{3,1,2,0:T(8,128)(2,1)S(1)}, u32[]{:S(2)}, u32[]{:S(2)}) collective-permute-start(bf16[2,512,2,128]{3,1,2,0:T(8,128)(2,1)S(1)} %get-tuple-element.515), channel_id=1, source_target_pairs={{0,4},{4,0},{1,5},{5,1},{2,6},{6,2},{3,7},{7,3},{8,12},{12,8},{9,1... | collective-permute-start | bytes 1572872 | tf_op jit(solution)/shard_map/while/body/eval_jaxpr/ppermute | solution.py:18
  171.4 4.3 %copy-start.2 = (f32[2,4,512,128]{3,2,1,0:T(8,128)S(1)}, f32[2,4,512,128]{3,2,1,0:T(8,128)}, u32[]{:S(2)}) copy-start(f32[2,4,512,128]{3,2,1,0:T(8,128)} %get-tuple-element.513) | copy-start | bytes 6291460
where the time goes:
time: 205 us
  matrix products  80.9 us (39%)
  waiting for transfers between devices  52.3 us (26%)
  starting transfers between devices  22.7 us (11%)
  other arithmetic  18.3 us (9%)
  blocking collectives  17.4 us (8%)
  local copies, waits for them, and re-layouts  12.1 us (6%)
    dot_general x8, matrix products, absorb(): jnp.einsum('kgts,skd->kgtd', weights, value_block.astype(jnp.float32), pr...  68.5 us
    ppermute x7, waiting for transfers between devices, passed_along(): return lax.ppermute(x, axis, [(i, (i + by) % size) for i in range(size)])  30.5 us
    all_to_all x1, blocking collectives, shards(): lax.all_to_all(result, 'head', split_axis=0, concat_axis=1, tiled=True)  17.4 us
    reduce_sum x4, other arithmetic, absorb(): run_sum = run_sum * factor + jnp.sum(weights, axis=-1)  16.4 us
    all_to_all x1, waiting for transfers between devices, shards(): lax.all_to_all(rotated_asking_matrix, 'head', split_axis=1, concat_axis=0...  14.2 us
    dot_general x8, matrix products, absorb(): jnp.einsum('tkgd,skd->kgts', grouped, key_block, preferred_element_type=j...  12.3 us
    ppermute x7, starting transfers between devices, passed_along(): return lax.ppermute(x, axis, [(i, (i + by) % size) for i in range(size)])  11.5 us
    unnamed x5, local copies, waits for them, and re-layouts  5.97 us
  transfers between devices with their start and end apart: 10, of which 7 were waited for; matrix products, arithmetic and copies ran while one was open for 39% of the time, Pallas kernels for 0%

commit v1 on v0

--- a/solution.py
+++ b/solution.py
@@ -19,8 +19,18 @@
 
 
 def shards(rotated_asking_matrix, rotated_lookup_matrix, content_matrix):
+
+    def serve_space(base_x, axis_id, dim_at, axis_no):
+        ready = jnp.concatenate(
+            lax.all_to_all(
+                jnp.stack(jnp.split(base_x, lax.axis_size(axis_id), dim_at), axis=0), axis_id, 0, 0
+            ),
+            axis=axis_no,
+        )
+        return ready
+
     query_local, key_local, value_local = (
-        lax.all_to_all(rotated_asking_matrix, "head", split_axis=1, concat_axis=0, tiled=True),
+        serve_space(rotated_asking_matrix, "head", 1, 0),
         lax.all_to_all(rotated_lookup_matrix, "head", split_axis=1, concat_axis=0, tiled=True),
         lax.all_to_all(content_matrix, "head", split_axis=1, concat_axis=0, tiled=True),
     )

time: 205 us -> 213 us (1.039)
  loops' own time: 0.47 us -> 8.34 us
    another operation x1, loops' own time: 0.47 us -> 8.34 us  [shards(): lax.fori_loop(0, outer_count - 1, outer_body, (carry, window))]
    unnamed x5 -> x4, local copies, waits for them, and re-layouts: 5.97 us -> 3.37 us
  transfers between devices with their start and end apart: 10 -> 10, of which waited for: 7 -> 7; matrix products, arithmetic and copies ran while one was open for 39% -> 38% of each run, Pallas kernels for 0% -> 0%
where the time goes in v1:
time: 213 us
  matrix products  80.9 us (38%)
  waiting for transfers between devices  52.5 us (25%)
  starting transfers between devices  22.7 us (11%)
  other arithmetic  19.4 us (9%)
  blocking collectives  17.4 us (8%)
  local copies, waits for them, and re-layouts  10.9 us (5%)
  loops' own time  8.34 us (4%)
    dot_general x8, matrix products, absorb(): jnp.einsum('kgts,skd->kgtd', weights, value_block.astype(jnp.float32), pr...  68.5 us
    ppermute x7, waiting for transfers between devices, passed_along(): return lax.ppermute(x, axis, [(i, (i + by) % size) for i in range(size)])  30.4 us
    all_to_all x1, blocking collectives, shards(): lax.all_to_all(result, 'head', split_axis=0, concat_axis=1, tiled=True)  17.4 us
    reduce_sum x4, other arithmetic, absorb(): run_sum = run_sum * factor + jnp.sum(weights, axis=-1)  16.4 us
    all_to_all x1, waiting for transfers between devices, serve_space(): lax.all_to_all(jnp.stack(jnp.split(base_x, lax.axis_size(axis_id), dim_at...  14.2 us
    dot_general x8, matrix products, absorb(): jnp.einsum('tkgd,skd->kgts', grouped, key_block, preferred_element_type=j...  12.3 us
    ppermute x7, starting transfers between devices, passed_along(): return lax.ppermute(x, axis, [(i, (i + by) % size) for i in range(size)])  11.5 us
    another operation x1, loops' own time, shards(): lax.fori_loop(0, outer_count - 1, outer_body, (carry, window))  8.34 us
  transfers between devices with their start and end apart: 10, of which 7 were waited for; matrix products, arithmetic and copies ran while one was open for 38% of the time, Pallas kernels for 0%

profile of v1, /device:TPU:0, one launch (start us, length us, event | category | flops | bytes accessed | tf_op | source)
XLA Modules:
  0.0 212.5 jit_solution(10583861661463919955)
XLA Ops:
  0.0 1.7 copy.14
  1.7 4.2 %all-to-all-start = ((bf16[128,8,128]{2,0,1:T(8,128)(2,1)}), bf16[128,8,128]{2,0,1:T(8,128)(2,1)S(1)}, u32[]{:S(2)}, u32[]{:S(2)}) async-start(bf16[128,8,128]{2,0,1:T(8,128)(2,1)} %copy.14), calls=%async_computation | async-start | bytes 524288 | tf_op jit(solution)/shard_map/all_to_all | solution.py:34
  5.9 1.7 copy.16
  7.6 4.3 %all-to-all-done = bf16[128,8,128]{2,0,1:T(8,128)(2,1)S(1)} async-done(((bf16[128,8,128]{2,0,1:T(8,128)(2,1)}), bf16[128,8,128]{2,0,1:T(8,128)(2,1)S(1)}, u32[]{:S(2)}, u32[]{:S(2)}) %all-to-all-start) | async-done | bytes 262176 | tf_op jit(solution)/shard_map/all_to_all | solution.py:34
  11.9 3.4 %all-to-all-start.1 = ((bf16[128,8,128]{2,0,1:T(8,128)(2,1)}), bf16[128,8,128]{2,0,1:T(8,128)(2,1)S(1)}, u32[]{:S(2)}, u32[]{:S(2)}) async-start(bf16[128,8,128]{2,0,1:T(8,128)(2,1)} %copy.16), calls=%async_computation.1 | async-start | bytes 524288 | tf_op jit(solution)/shard_map/all_to_all | solution.py:35
  17.7 3.6 %all-to-all-done.1 = bf16[128,8,128]{2,0,1:T(8,128)(2,1)S(1)} async-done(((bf16[128,8,128]{2,0,1:T(8,128)(2,1)}), bf16[128,8,128]{2,0,1:T(8,128)(2,1)S(1)}, u32[]{:S(2)}, u32[]{:S(2)}) %all-to-all-start.1) | async-done | bytes 262176 | tf_op jit(solution)/shard_map/all_to_all | solution.py:35
  21.3 3.5 %all-to-all-start.2 = ((bf16[4,128,8,128]{3,2,1,0:T(8,128)(2,1)}), bf16[4,128,8,128]{3,2,1,0:T(8,128)(2,1)S(1)}, u32[]{:S(2)}, u32[]{:S(2)}) async-start(bf16[4,128,8,128]{3,2,1,0:T(8,128)(2,1)} %pad_maximum_fusion), calls=%async_computation.2 | async-start | bytes 2097152 | tf_op jit(solution)/shard_map/all_to_all | solution.py:25
  25.1 14.2 %all-to-all-done.2 = bf16[4,128,8,128]{3,2,1,0:T(8,128)(2,1)S(1)} async-done(((bf16[4,128,8,128]{3,2,1,0:T(8,128)(2,1)}), bf16[4,128,8,128]{3,2,1,0:T(8,128)(2,1)S(1)}, u32[]{:S(2)}, u32[]{:S(2)}) %all-to-all-start.2) | async-done | bytes 1048608 | tf_op jit(solution)/shard_map/all_to_all | solution.py:25
  39.5 119.6 %while.49 = (s32[]{:T(128)}, f32[2,4,512]{2,1,0:T(4,128)S(1)}, f32[2,4,512]{2,1,0:T(4,128)S(1)}, f32[2,4,512,128]{3,2,1,0:T(8,128)}, bf16[2,512,2,128]{3,1,2,0:T...) while((s32[]{:T(128)}, f32[2,4,512]{2,1,0:T(4,128)S(1)}, ...), condition=%wide.region_5.6_spmd.clone.clone, body=%wide.region_0.5_spmd.clone.clone.sunk | while | flops 7569716736 | bytes 86422968 | solution.py:116
  39.5 2.2 %collective-permute-start = (bf16[2,512,2,128]{3,1,2,0:T(8,128)(2,1)S(1)}, bf16[2,512,2,128]{3,1,2,0:T(8,128)(2,1)S(1)}, u32[]{:S(2)}, u32[]{:S(2)}) collective-permute-start(bf16[2,512,2,128]{3,1,2,0:T(8,128)(2,1)S(1)} %copy.46), channel_id=1, source_target_pairs={{0,4},{4,0},{1,5},{5,1},{2,6},{6,2},{3,7},{7,3},{8,12},{12,8},{9,1... | collective-permute-start | bytes 1572872 | tf_op jit(solution)/shard_map/while/body/eval_jaxpr/while/body/eval_jaxpr/ppermute | solution.py:18
  41.7 1.6 collective-permute-start.1
  45.3 8.1 %collective-permute-done = bf16[2,512,2,128]{3,1,2,0:T(8,128)(2,1)S(1)} collective-permute-done((bf16[2,512,2,128]{3,1,2,0:T(8,128)(2,1)S(1)}, bf16[2,512,2,128]{3,1,2,0:T(8,128)(2,1)S(1)}, u32[]{:S(2)}, u32[]{:S(2)}) %collective-permute-start) | collective-permute-done | bytes 524320 | tf_op jit(solution)/shard_map/while/body/eval_jaxpr/while/body/eval_jaxpr/ppermute | solution.py:18
  54.9 7.6 %fusion.117 = f32[2,4,512,128]{3,2,1,0:T(8,128)S(1)} fusion(f32[2,512,512,4]{2,1,3,0:T(8,128)S(1)} %get-tuple-element.744, f32[2,4,512]{2,1,0:T(4,128)S(1)} %get-tuple-element.745, pred[512,512]{0,1:T(8,128)(4,1)S(1)} %get-tuple-element.741, bf16[2,512,2,128]{3,1,2,0:T(8,128)(2,1)S(1)} %copy.46), kind=kOutput, calls=%fused_computation.11.clone.1 | convolution fusion | flops 3229614080 | bytes 11026432 | tf_op jit(solution)/shard_map/while/body/eval_jaxpr/kgts,skd->kgtd/dot_general | solution.py:68
  62.6 4.1 %fusion.115 = (f32[2,4,512]{2,1,0:T(4,128)S(1)}, f32[2,4,512]{2,1,0:T(4,128)S(1)}) fusion(f32[2,512,512,4]{2,1,3,0:T(8,128)S(1)} %get-tuple-element.744, f32[2,4,512]{2,1,0:T(4,128)S(1)} %get-tuple-element.745, pred[512,512]{0,1:T(8,128)(4,1)S(1)} %get-tuple-element.741, f32[2,4,512]{2,1,0:T(4,128)S(1)} %get-tuple-element.781, ...), kind=kLoop, calls=%fused_computation.12.clone.1 | loop fusion | flops 20963328 | bytes 17367040 | tf_op jit(solution)/shard_map/while/body/eval_jaxpr/reduce_sum | solution.py:67
  66.7 9.6 %fusion.118 = f32[2,4,512,128]{3,2,1,0:T(8,128)S(1)} fusion(f32[2,4,512,128]{3,2,1,0:T(8,128)S(1)} %fusion.117, f32[2,4,512,128]{3,2,1,0:T(8,128)S(1)} %copy-done, f32[2,512,512,4]{2,1,3,0:T(8,128)S(1)} %get-tuple-element.746, f32[2,4,512]{2,1,0:T(4,128)S(1)} %get-tuple-element.781, pred[512,512]{0,1:T(8,128)(4,1)S(1)} %get-tuple-element.739, ...), kind=kOutput, calls=%fused_computation.28.clone.1 | convolution fusion | flops 3232235520 | bytes 15253505 | tf_op jit(solution)/shard_map/while/body/eval_jaxpr/while/body/eval_jaxpr/kgts,skd->kgtd/dot_general | solution.py:68
  77.7 1.8 collective-permute-start
  79.5 1.6 collective-permute-start.1
  81.5 1.5 fusion.113
  83.0 7.5 %collective-permute-done = bf16[2,512,2,128]{3,1,2,0:T(8,128)(2,1)S(1)} collective-permute-done((bf16[2,512,2,128]{3,1,2,0:T(8,128)(2,1)S(1)}, bf16[2,512,2,128]{3,1,2,0:T(8,128)(2,1)S(1)}, u32[]{:S(2)}, u32[]{:S(2)}) %collective-permute-start) | collective-permute-done | bytes 524320 | tf_op jit(solution)/shard_map/while/body/eval_jaxpr/while/body/eval_jaxpr/ppermute | solution.py:18
  92.1 7.6 %fusion.117 = f32[2,4,512,128]{3,2,1,0:T(8,128)S(1)} fusion(f32[2,512,512,4]{2,1,3,0:T(8,128)S(1)} %get-tuple-element.744, f32[2,4,512]{2,1,0:T(4,128)S(1)} %get-tuple-element.745, pred[512,512]{0,1:T(8,128)(4,1)S(1)} %get-tuple-element.741, bf16[2,512,2,128]{3,1,2,0:T(8,128)(2,1)S(1)} %copy.46), kind=kOutput, calls=%fused_computation.11.clone.1 | convolution fusion | flops 3229614080 | bytes 11026432 | tf_op jit(solution)/shard_map/while/body/eval_jaxpr/kgts,skd->kgtd/dot_general | solution.py:68
  99.7 4.1 %fusion.115 = (f32[2,4,512]{2,1,0:T(4,128)S(1)}, f32[2,4,512]{2,1,0:T(4,128)S(1)}) fusion(f32[2,512,512,4]{2,1,3,0:T(8,128)S(1)} %get-tuple-element.744, f32[2,4,512]{2,1,0:T(4,128)S(1)} %get-tuple-element.745, pred[512,512]{0,1:T(8,128)(4,1)S(1)} %get-tuple-element.741, f32[2,4,512]{2,1,0:T(4,128)S(1)} %get-tuple-element.781, ...), kind=kLoop, calls=%fused_computation.12.clone.1 | loop fusion | flops 20963328 | bytes 17367040 | tf_op jit(solution)/shard_map/while/body/eval_jaxpr/reduce_sum | solution.py:67
  103.8 9.6 %fusion.118 = f32[2,4,512,128]{3,2,1,0:T(8,128)S(1)} fusion(f32[2,4,512,128]{3,2,1,0:T(8,128)S(1)} %fusion.117, f32[2,4,512,128]{3,2,1,0:T(8,128)S(1)} %copy-done, f32[2,512,512,4]{2,1,3,0:T(8,128)S(1)} %get-tuple-element.746, f32[2,4,512]{2,1,0:T(4,128)S(1)} %get-tuple-element.781, pred[512,512]{0,1:T(8,128)(4,1)S(1)} %get-tuple-element.739, ...), kind=kOutput, calls=%fused_computation.28.clone.1 | convolution fusion | flops 3232235520 | bytes 15253505 | tf_op jit(solution)/shard_map/while/body/eval_jaxpr/while/body/eval_jaxpr/kgts,skd->kgtd/dot_general | solution.py:68
  116.3 1.6 collective-permute-start.1
  119.9 6.9 %collective-permute-done = bf16[2,512,2,128]{3,1,2,0:T(8,128)(2,1)S(1)} collective-permute-done((bf16[2,512,2,128]{3,1,2,0:T(8,128)(2,1)S(1)}, bf16[2,512,2,128]{3,1,2,0:T(8,128)(2,1)S(1)}, u32[]{:S(2)}, u32[]{:S(2)}) %collective-permute-start) | collective-permute-done | bytes 524320 | tf_op jit(solution)/shard_map/while/body/eval_jaxpr/while/body/eval_jaxpr/ppermute | solution.py:18
  128.4 7.6 %fusion.117 = f32[2,4,512,128]{3,2,1,0:T(8,128)S(1)} fusion(f32[2,512,512,4]{2,1,3,0:T(8,128)S(1)} %get-tuple-element.744, f32[2,4,512]{2,1,0:T(4,128)S(1)} %get-tuple-element.745, pred[512,512]{0,1:T(8,128)(4,1)S(1)} %get-tuple-element.741, bf16[2,512,2,128]{3,1,2,0:T(8,128)(2,1)S(1)} %copy.46), kind=kOutput, calls=%fused_computation.11.clone.1 | convolution fusion | flops 3229614080 | bytes 11026432 | tf_op jit(solution)/shard_map/while/body/eval_jaxpr/kgts,skd->kgtd/dot_general | solution.py:68
  136.0 4.1 %fusion.115 = (f32[2,4,512]{2,1,0:T(4,128)S(1)}, f32[2,4,512]{2,1,0:T(4,128)S(1)}) fusion(f32[2,512,512,4]{2,1,3,0:T(8,128)S(1)} %get-tuple-element.744, f32[2,4,512]{2,1,0:T(4,128)S(1)} %get-tuple-element.745, pred[512,512]{0,1:T(8,128)(4,1)S(1)} %get-tuple-element.741, f32[2,4,512]{2,1,0:T(4,128)S(1)} %get-tuple-element.781, ...), kind=kLoop, calls=%fused_computation.12.clone.1 | loop fusion | flops 20963328 | bytes 17367040 | tf_op jit(solution)/shard_map/while/body/eval_jaxpr/reduce_sum | solution.py:67
  140.1 9.6 %fusion.118 = f32[2,4,512,128]{3,2,1,0:T(8,128)S(1)} fusion(f32[2,4,512,128]{3,2,1,0:T(8,128)S(1)} %fusion.117, f32[2,4,512,128]{3,2,1,0:T(8,128)S(1)} %copy-done, f32[2,512,512,4]{2,1,3,0:T(8,128)S(1)} %get-tuple-element.746, f32[2,4,512]{2,1,0:T(4,128)S(1)} %get-tuple-element.781, pred[512,512]{0,1:T(8,128)(4,1)S(1)} %get-tuple-element.739, ...), kind=kOutput, calls=%fused_computation.28.clone.1 | convolution fusion | flops 3232235520 | bytes 15253505 | tf_op jit(solution)/shard_map/while/body/eval_jaxpr/while/body/eval_jaxpr/kgts,skd->kgtd/dot_general | solution.py:68
  162.2 8.0 %collective-permute-done.2 = bf16[2,512,2,128]{3,1,2,0:T(8,128)(2,1)S(1)} collective-permute-done((bf16[2,512,2,128]{3,1,2,0:T(8,128)(2,1)S(1)}, bf16[2,512,2,128]{3,1,2,0:T(8,128)(2,1)S(1)}, u32[]{:S(2)}, u32[]{:S(2)}) %collective-permute-start.2) | collective-permute-done | bytes 524320 | tf_op jit(solution)/shard_map/while/body/eval_jaxpr/ppermute | solution.py:18
  171.8 7.6 %fusion.58 = f32[2,4,512,128]{3,2,1,0:T(8,128)S(1)} fusion(f32[2,512,512,4]{2,1,3,0:T(8,128)S(1)} %get-tuple-element.653, f32[2,4,512]{2,1,0:T(4,128)S(1)} %bitcast.175, pred[512,512]{0,1:T(8,128)(4,1)S(1)} %get-tuple-element.648, bf16[2,512,2,128]{3,1,2,0:T(8,128)(2,1)S(1)} %get-tuple-element.515), kind=kOutput, calls=%fused_computation.78 | convolution fusion | flops 3229614080 | bytes 11026432 | tf_op jit(solution)/shard_map/kgts,skd->kgtd/dot_general | solution.py:68
  179.4 4.2 %fusion.57 = (f32[2,4,512]{2,1,0:T(4,128)S(1)}, f32[2,4,512]{2,1,0:T(4,128)S(1)}) fusion(f32[2,512,512,4]{2,1,3,0:T(8,128)S(1)} %get-tuple-element.653, f32[2,4,512]{2,1,0:T(4,128)S(1)} %bitcast.176, pred[512,512]{0,1:T(8,128)(4,1)S(1)} %get-tuple-element.648, f32[2,4,512]{2,1,0:T(4,128)S(1)} %bitcast.173, f32[2,512,512,4]{2,1,3,0:T(8,128)S(1)} %get-tuple-element.651, ...), kind=kLoop, calls=%fused_computation.77 | loop fusion | flops 20963328 | bytes 17367040 | tf_op jit(solution)/shard_map/reduce_sum | solution.py:67
  183.6 9.4 %divide_convert_fusion = bf16[2,4,512,128]{3,2,1,0:T(8,128)(2,1)S(1)} fusion(f32[2,4,512,128]{3,2,1,0:T(8,128)S(1)} %fusion.58, f32[2,4,512,128]{3,2,1,0:T(8,128)S(1)} %copy-done.2, f32[2,512,512,4]{2,1,3,0:T(8,128)S(1)} %get-tuple-element.651, f32[2,4,512]{2,1,0:T(4,128)S(1)} %bitcast.174, pred[512,512]{0,1:T(8,128)(4,1)S(1)} %get-tuple-element.649, ...), kind=kOutput, calls=%fused_computation.91 | convolution fusion | flops 3232759808 | bytes 14221312 | tf_op jit(solution)/shard_map/while/body/eval_jaxpr/kgts,skd->kgtd/dot_general | solution.py:68
  193.7 17.4 %all_to_all.53 = bf16[512,8,128]{2,1,0:T(8,128)(2,1)S(1)} all-to-all(bf16[512,8,128]{2,1,0:T(8,128)(2,1)S(1)} %copy.21), channel_id=1, replica_groups=mesh['head'=4,'inner'=2,'outer'=4] {'head'}, dimensions={0} | all-to-all | bytes 2097152 | tf_op jit(solution)/shard_map/all_to_all | solution.py:121
  (67 shorter events, 24.0 us)
Async XLA Ops:
  1.7 10.2 %all-to-all-start = ((bf16[128,8,128]{2,0,1:T(8,128)(2,1)}), bf16[128,8,128]{2,0,1:T(8,128)(2,1)S(1)}, u32[]{:S(2)}, u32[]{:S(2)}) async-start(bf16[128,8,128]{2,0,1:T(8,128)(2,1)} %copy.14), calls=%async_computation | async-start | bytes 524288 | tf_op jit(solution)/shard_map/all_to_all | solution.py:34
  11.9 9.4 %all-to-all-start.1 = ((bf16[128,8,128]{2,0,1:T(8,128)(2,1)}), bf16[128,8,128]{2,0,1:T(8,128)(2,1)S(1)}, u32[]{:S(2)}, u32[]{:S(2)}) async-start(bf16[128,8,128]{2,0,1:T(8,128)(2,1)} %copy.16), calls=%async_computation.1 | async-start | bytes 524288 | tf_op jit(solution)/shard_map/all_to_all | solution.py:35
  21.3 17.9 %all-to-all-start.2 = ((bf16[4,128,8,128]{3,2,1,0:T(8,128)(2,1)}), bf16[4,128,8,128]{3,2,1,0:T(8,128)(2,1)S(1)}, u32[]{:S(2)}, u32[]{:S(2)}) async-start(bf16[4,128,8,128]{3,2,1,0:T(8,128)(2,1)} %pad_maximum_fusion), calls=%async_computation.2 | async-start | bytes 2097152 | tf_op jit(solution)/shard_map/all_to_all | solution.py:25
  39.5 13.8 %collective-permute-start = (bf16[2,512,2,128]{3,1,2,0:T(8,128)(2,1)S(1)}, bf16[2,512,2,128]{3,1,2,0:T(8,128)(2,1)S(1)}, u32[]{:S(2)}, u32[]{:S(2)}) collective-permute-start(bf16[2,512,2,128]{3,1,2,0:T(8,128)(2,1)S(1)} %copy.46), channel_id=1, source_target_pairs={{0,4},{4,0},{1,5},{5,1},{2,6},{6,2},{3,7},{7,3},{8,12},{12,8},{9,1... | collective-permute-start | bytes 1572872 | tf_op jit(solution)/shard_map/while/body/eval_jaxpr/while/body/eval_jaxpr/ppermute | solution.py:18
  41.7 34.5 %collective-permute-start.1 = (bf16[2,512,2,128]{3,1,2,0:T(8,128)(2,1)S(1)}, bf16[2,512,2,128]{3,1,2,0:T(8,128)(2,1)S(1)}, u32[]{:S(2)}, u32[]{:S(2)}) collective-permute-start(bf16[2,512,2,128]{3,1,2,0:T(8,128)(2,1)S(1)} %copy.46), channel_id=1, source_target_pairs={{0,1},{1,2},{2,3},{3,0},{4,5},{5,6},{6,7},{7,4},{8,9},{9,10},{10,1... | collective-permute-start | bytes 1572872 | tf_op jit(solution)/shard_map/while/body/eval_jaxpr/ppermute | solution.py:18
  62.6 4.1 %copy-start = (f32[2,4,512,128]{3,2,1,0:T(8,128)S(1)}, f32[2,4,512,128]{3,2,1,0:T(8,128)}, u32[]{:S(2)}) copy-start(f32[2,4,512,128]{3,2,1,0:T(8,128)} %get-tuple-element.769) | copy-start | bytes 6291460 | tf_op jit(solution)/shard_map/while
  76.3 1.3 copy-start.1
  77.7 12.9 %collective-permute-start = (bf16[2,512,2,128]{3,1,2,0:T(8,128)(2,1)S(1)}, bf16[2,512,2,128]{3,1,2,0:T(8,128)(2,1)S(1)}, u32[]{:S(2)}, u32[]{:S(2)}) collective-permute-start(bf16[2,512,2,128]{3,1,2,0:T(8,128)(2,1)S(1)} %copy.46), channel_id=1, source_target_pairs={{0,4},{4,0},{1,5},{5,1},{2,6},{6,2},{3,7},{7,3},{8,12},{12,8},{9,1... | collective-permute-start | bytes 1572872 | tf_op jit(solution)/shard_map/while/body/eval_jaxpr/while/body/eval_jaxpr/ppermute | solution.py:18
  79.5 34.0 %collective-permute-start.1 = (bf16[2,512,2,128]{3,1,2,0:T(8,128)(2,1)S(1)}, bf16[2,512,2,128]{3,1,2,0:T(8,128)(2,1)S(1)}, u32[]{:S(2)}, u32[]{:S(2)}) collective-permute-start(bf16[2,512,2,128]{3,1,2,0:T(8,128)(2,1)S(1)} %copy.46), channel_id=1, source_target_pairs={{0,1},{1,2},{2,3},{3,0},{4,5},{5,6},{6,7},{7,4},{8,9},{9,10},{10,1... | collective-permute-start | bytes 1572872 | tf_op jit(solution)/shard_map/while/body/eval_jaxpr/ppermute | solution.py:18
  99.7 4.1 %copy-start = (f32[2,4,512,128]{3,2,1,0:T(8,128)S(1)}, f32[2,4,512,128]{3,2,1,0:T(8,128)}, u32[]{:S(2)}) copy-start(f32[2,4,512,128]{3,2,1,0:T(8,128)} %get-tuple-element.769) | copy-start | bytes 6291460 | tf_op jit(solution)/shard_map/while
  113.4 1.3 copy-start.1
  114.8 12.0 %collective-permute-start = (bf16[2,512,2,128]{3,1,2,0:T(8,128)(2,1)S(1)}, bf16[2,512,2,128]{3,1,2,0:T(8,128)(2,1)S(1)}, u32[]{:S(2)}, u32[]{:S(2)}) collective-permute-start(bf16[2,512,2,128]{3,1,2,0:T(8,128)(2,1)S(1)} %copy.46), channel_id=1, source_target_pairs={{0,4},{4,0},{1,5},{5,1},{2,6},{6,2},{3,7},{7,3},{8,12},{12,8},{9,1... | collective-permute-start | bytes 1572872 | tf_op jit(solution)/shard_map/while/body/eval_jaxpr/while/body/eval_jaxpr/ppermute | solution.py:18
  116.3 33.4 %collective-permute-start.1 = (bf16[2,512,2,128]{3,1,2,0:T(8,128)(2,1)S(1)}, bf16[2,512,2,128]{3,1,2,0:T(8,128)(2,1)S(1)}, u32[]{:S(2)}, u32[]{:S(2)}) collective-permute-start(bf16[2,512,2,128]{3,1,2,0:T(8,128)(2,1)S(1)} %copy.46), channel_id=1, source_target_pairs={{0,1},{1,2},{2,3},{3,0},{4,5},{5,6},{6,7},{7,4},{8,9},{9,10},{10,1... | collective-permute-start | bytes 1572872 | tf_op jit(solution)/shard_map/while/body/eval_jaxpr/ppermute | solution.py:18
  136.0 4.1 %copy-start = (f32[2,4,512,128]{3,2,1,0:T(8,128)S(1)}, f32[2,4,512,128]{3,2,1,0:T(8,128)}, u32[]{:S(2)}) copy-start(f32[2,4,512,128]{3,2,1,0:T(8,128)} %get-tuple-element.769) | copy-start | bytes 6291460 | tf_op jit(solution)/shard_map/while
  149.7 1.3 copy-start.1
  159.1 11.1 %collective-permute-start.2 = (bf16[2,512,2,128]{3,1,2,0:T(8,128)(2,1)S(1)}, bf16[2,512,2,128]{3,1,2,0:T(8,128)(2,1)S(1)}, u32[]{:S(2)}, u32[]{:S(2)}) collective-permute-start(bf16[2,512,2,128]{3,1,2,0:T(8,128)(2,1)S(1)} %get-tuple-element.515), channel_id=1, source_target_pairs={{0,4},{4,0},{1,5},{5,1},{2,6},{6,2},{3,7},{7,3},{8,12},{12,8},{9,1... | collective-permute-start | bytes 1572872 | tf_op jit(solution)/shard_map/while/body/eval_jaxpr/ppermute | solution.py:18
  179.4 4.3 %copy-start.2 = (f32[2,4,512,128]{3,2,1,0:T(8,128)S(1)}, f32[2,4,512,128]{3,2,1,0:T(8,128)}, u32[]{:S(2)}) copy-start(f32[2,4,512,128]{3,2,1,0:T(8,128)} %get-tuple-element.513) | copy-start | bytes 6291460
